TPU v7x, 32 devices: a whole 2x2x4 slice. The times are simulated.
32 devices in a mesh: ep: 4 (over z), fsdp: 8 (over y, x, core).
Axes of the slice: x: 2, y: 2, z: 4, core: 2. Of those that a mesh axis runs over, the one named last changes fastest.
Arguments:
- train_gate: float32 [64, 2048, 1408], P('ep', 'fsdp'), may hold values from -0.1875 to 0.1875
- train_up: float32 [64, 2048, 1408], P('ep', 'fsdp'), may hold values from -0.1875 to 0.1875
- train_down: float32 [64, 1408, 2048], P('ep', None, 'fsdp'), may hold values from -0.21875 to 0.21875
- router_weight: float32 [2048, 64], P('fsdp', 'ep'), may hold values from -0.125 to 0.125
- router_gain: float32 [2048], P('fsdp'), may hold values from 0.25 to 1.75
Outputs:
- ready_gate: bfloat16 [64, 2048, 1408], P('ep', None, 'fsdp')
- ready_up: bfloat16 [64, 2048, 1408], P('ep', None, 'fsdp')
- ready_down: bfloat16 [64, 1408, 2048], P('ep', 'fsdp')
- scale_gate: float32 [64, 1408], P('ep', 'fsdp')
- scale_up: float32 [64, 1408], P('ep', 'fsdp')
- scale_down: float32 [64, 1408], P('ep', 'fsdp')
- serve_router: bfloat16 [2048, 64], replicated
All inputs are finite; a program needn't handle non-finite values. Where the computation divides by a largest or mean magnitude, that divisor is 1e-20 or more.
Results may differ from a plain program's by a relative error of at most 0.012.
Values may be sent and summed in bfloat16 or wider, within the bound.
A program may use at most 192 MiB of HBM per device.

v0:
```python
import jax
import jax.numpy as jnp
from jax import lax
from jax.sharding import PartitionSpec as P

D_MODEL = 2048


def shards(train_gate, train_up, train_down, router_weight, router_gain):
    total_gate, total_up, total_down = (
        lax.psum(jnp.sum(jnp.abs(train_gate), axis=1).astype(jnp.bfloat16), "fsdp").astype(
            jnp.float32
        ),
        lax.psum(jnp.sum(jnp.abs(train_up), axis=1).astype(jnp.bfloat16), "fsdp").astype(
            jnp.float32
        ),
        lax.psum(jnp.sum(jnp.abs(train_down), axis=2).astype(jnp.bfloat16), "fsdp").astype(
            jnp.float32
        ),
    )
    scale_gate = total_gate / D_MODEL
    scale_up = total_up / D_MODEL
    scale_down = total_down / D_MODEL
    narrow_gate, narrow_up, narrow_down = (
        (train_gate / jnp.expand_dims(scale_gate, 1)).astype(jnp.bfloat16),
        (train_up / jnp.expand_dims(scale_up, 1)).astype(jnp.bfloat16),
        (train_down / jnp.expand_dims(scale_down, 2)).astype(jnp.bfloat16),
    )
    ready_gate, ready_up = (
        lax.all_to_all(narrow_gate, "fsdp", split_axis=2, concat_axis=1, tiled=True),
        lax.all_to_all(narrow_up, "fsdp", split_axis=2, concat_axis=1, tiled=True),
    )
    ready_down = lax.all_to_all(narrow_down, "fsdp", split_axis=1, concat_axis=2, tiled=True)
    scale_gate = lax.dynamic_slice_in_dim(
        scale_gate, lax.axis_index("fsdp") * ready_gate.shape[2], ready_gate.shape[2], axis=1
    )
    scale_up = lax.dynamic_slice_in_dim(
        scale_up, lax.axis_index("fsdp") * ready_up.shape[2], ready_up.shape[2], axis=1
    )
    scale_down = lax.dynamic_slice_in_dim(
        scale_down, lax.axis_index("fsdp") * ready_down.shape[1], ready_down.shape[1], axis=1
    )
    part_router = (router_weight * router_gain[:, None]).astype(jnp.bfloat16)
    row_router = lax.all_gather(part_router, "fsdp", axis=0, tiled=True)
    serve_router = lax.all_gather(row_router, "ep", axis=1, tiled=True)
    return (ready_gate, ready_up, ready_down, scale_gate, scale_up, scale_down, serve_router)


def solution(mesh):
    in_specs = (
        P("ep", "fsdp", None),
        P("ep", "fsdp", None),
        P("ep", None, "fsdp"),
        P("fsdp", "ep"),
        P("fsdp"),
    )
    out_specs = (
        P("ep", None, "fsdp"),
        P("ep", None, "fsdp"),
        P("ep", "fsdp", None),
        P("ep", "fsdp"),
        P("ep", "fsdp"),
        P("ep", "fsdp"),
        P(),
    )
    return jax.shard_map(shards, mesh=mesh, in_specs=in_specs, out_specs=out_specs, check_vma=False)
```

profile of v0, /device:TPU:0, one launch (start us, length us, event | category | flops | bytes accessed | tf_op | source)
XLA Modules:
  0.0 617.4 jit_solution(11987987628351158617)
XLA Ops:
  7.2 0.0 all-reduce.3.cloned.1.call-start
  7.2 0.0 copy-start
  7.2 9.2 %abs_reduce_fusion = bf16[16,1408]{1,0:T(8,128)(2,1)} fusion(f32[16,1408,256]{2,1,0:T(8,128)} %param.7), kind=kLoop, calls=%fused_computation.2 | loop fusion | flops 11511808 | bytes 23113728 | tf_op jit(solution)/shard_map/reduce_sum | solution.py:17
  16.4 5.0 copy-done
  21.4 11.7 %abs_reduce_fusion.1 = (bf16[16,1408]{1,0:T(8,128)(2,1)}, bf16[16,1408]{1,0:T(8,128)(2,1)}) fusion(f32[16,256,1408]{2,1,0:T(8,128)S(1)} %copy-done, f32[16,256,1408]{2,1,0:T(8,128)} %param.5), kind=kLoop, calls=%fused_computation.4 | loop fusion | flops 23023616 | bytes 46227456 | tf_op jit(solution)/shard_map/reduce_sum | solution.py:14
  33.1 0.0 all-reduce.3.cloned.1.call-update
  33.1 23.7 %copy.28 = f32[16,256,1408]{1,0,2:T(8,128)} copy(f32[16,256,1408]{2,1,0:T(8,128)} %param.6) | data formatting | bytes 46137344 | tf_op args[1]
  56.8 31.4 %all-reduce.3.cloned.1.call-done = (bf16[16,1408]{1,0:T(8,128)(2,1)}, bf16[16,1408]{1,0:T(8,128)(2,1)}, bf16[16,1408]{1,0:T(8,128)(2,1)}) async-done(((bf16[16,1408]{1,0:T(8,128)(2,1)}, bf16[16,1408]{1,0:T(8,128)(2,1)}, bf16[16,1408]{1,0:T(8,128)(2,1)}), (bf16[16,1408]{1,0:T(8,128)(2,1)}, bf16[16,1408]{1,0:T(8,128)(2,1)}, bf16[16,1408]{1,0:T(8,128)(2,1)})) %all-reduce.3.cloned.1.call-update) | async-done | bytes 135184 | tf_op jit(solution)/shard_map/psum | solution.py:11
  88.3 0.8 convert_multiply_fusion.1
  89.1 0.3 copy.27
  89.3 14.2 %divide_convert_fusion = bf16[16,256,1408]{1,0,2:T(8,128)(2,1)} fusion(f32[16,256,1408]{1,0,2:T(8,128)} %copy.28, f32[16,1408]{0,1:T(8,128)S(1)} %copy.27), kind=kLoop, calls=%fused_computation.3 | loop fusion | flops 11534336 | bytes 34693120 | tf_op jit(solution)/shard_map/convert_element_type | solution.py:26
  103.5 5.2 all-to-all-start.1
  108.8 0.0 copy-start.2
  108.8 23.7 %copy.24 = f32[16,256,1408]{1,0,2:T(8,128)} copy(f32[16,256,1408]{2,1,0:T(8,128)} %param.5) | data formatting | bytes 46137344 | tf_op args[0]
  132.5 0.0 copy-done.2
  132.5 0.3 copy.23
  132.8 0.0 copy-start.1
  132.8 14.2 %divide_convert_fusion.1 = bf16[16,256,1408]{1,0,2:T(8,128)(2,1)} fusion(f32[16,256,1408]{1,0,2:T(8,128)} %copy.24, f32[16,1408]{0,1:T(8,128)S(1)} %copy.23), kind=kLoop, calls=%fused_computation.5 | loop fusion | flops 11534336 | bytes 34693120 | tf_op jit(solution)/shard_map/convert_element_type | solution.py:25
  147.0 89.5 %all-to-all-done.1 = bf16[16,256,1408]{1,0,2:T(8,128)(2,1)} async-done(((bf16[16,256,1408]{1,0,2:T(8,128)(2,1)}), bf16[16,256,1408]{1,0,2:T(8,128)(2,1)}, u32[]{:S(2)}, u32[]{:S(2)}) %all-to-all-start.1) | async-done | bytes 11534368 | tf_op jit(solution)/shard_map/all_to_all | solution.py:31
  236.5 5.3 all-to-all-start
  241.8 0.0 copy-done.1
  241.8 0.3 copy.31
  242.1 0.0 copy-start.3
  242.1 0.0 copy-start.4
  242.1 32.6 %fusion = bf16[16,1408,256]{2,0,1:T(8,128)(2,1)} fusion(f32[16,1408,256]{2,1,0:T(8,128)} %param.7, f32[16,1408]{0,1:T(8,128)S(1)} %copy.31), kind=kLoop, calls=%fused_computation.1 | loop fusion | flops 11534336 | bytes 34693120 | tf_op jit(solution)/shard_map/convert_element_type | solution.py:27
  274.7 94.8 %all-to-all-done = bf16[16,256,1408]{1,0,2:T(8,128)(2,1)} async-done(((bf16[16,256,1408]{1,0,2:T(8,128)(2,1)}), bf16[16,256,1408]{1,0,2:T(8,128)(2,1)}, u32[]{:S(2)}, u32[]{:S(2)}) %all-to-all-start) | async-done | bytes 11534368 | tf_op jit(solution)/shard_map/all_to_all | solution.py:30
  369.6 5.3 all-to-all-start.2
  374.8 0.0 copy-done.3
  374.8 0.0 copy-done.4
  374.9 130.9 %all_gather.6 = bf16[2048,16]{0,1:T(8,128)(2,1)S(1)} all-gather(bf16[256,16]{0,1:T(8,128)(2,1)S(1)} %multiply_convert_fusion), channel_id=1, replica_groups=mesh['ep'=4,'fsdp'=8] {'fsdp'}, dimensions={0}, use_global_device_ids=true | all-gather | bytes 73728 | tf_op jit(solution)/shard_map/all_gather | solution.py:44
  505.8 14.2 %all_gather.7 = bf16[2048,64]{0,1:T(8,128)(2,1)S(1)} all-gather(bf16[2048,16]{0,1:T(8,128)(2,1)S(1)} %all_gather.6), channel_id=1, replica_groups=mesh['ep'=4,'fsdp'=8] {'ep'}, dimensions={1}, use_global_device_ids=true | all-gather | bytes 327680 | tf_op jit(solution)/shard_map/all_gather | solution.py:45
  519.9 0.7 constant_dynamic-slice_fusion
  520.6 0.7 constant_dynamic-slice_fusion.1
  521.3 0.7 constant_dynamic-slice_fusion.2
  522.0 11.3 %copy.30 = bf16[16,8,256,176]{2,1,3,0:T(8,128)(2,1)} copy(bf16[16,8,256,176]{2,0,3,1:T(8,128)(2,1)} %bitcast.5) | data formatting | bytes 23068672 | tf_op jit(solution)/shard_map/all_to_all | solution.py:31
  533.3 18.0 %all_to_all.46 = bf16[16,2048,176]{1,2,0:T(8,128)(2,1)} reshape(bf16[16,8,256,176]{2,1,3,0:T(8,128)(2,1)} %copy.30) | data formatting | bytes 23068672 | tf_op jit(solution)/shard_map/all_to_all | solution.py:31
  551.3 11.3 %copy.26 = bf16[16,8,256,176]{2,1,3,0:T(8,128)(2,1)} copy(bf16[16,8,256,176]{2,0,3,1:T(8,128)(2,1)} %bitcast.2) | data formatting | bytes 23068672 | tf_op jit(solution)/shard_map/all_to_all | solution.py:30
  562.6 18.0 %all_to_all.42 = bf16[16,2048,176]{1,2,0:T(8,128)(2,1)} reshape(bf16[16,8,256,176]{2,1,3,0:T(8,128)(2,1)} %copy.26) | data formatting | bytes 23068672 | tf_op jit(solution)/shard_map/all_to_all | solution.py:30
  580.6 0.0 all-to-all-done.2
  580.6 11.3 %copy.33 = bf16[16,176,8,256]{3,2,1,0:T(8,128)(2,1)} copy(bf16[16,176,8,256]{3,0,1,2:T(8,128)(2,1)} %bitcast.7) | data formatting | bytes 23068672 | tf_op jit(solution)/shard_map/all_to_all | solution.py:33
  591.9 18.0 %all_to_all.50 = bf16[16,176,2048]{2,1,0:T(8,128)(2,1)} reshape(bf16[16,176,8,256]{3,2,1,0:T(8,128)(2,1)} %copy.33) | data formatting | bytes 23068672 | tf_op jit(solution)/shard_map/all_to_all | solution.py:33
  609.9 0.7 copy.43
  (3 shorter events, 0.0 us)
Async XLA Ops:
  7.2 81.1 %all-reduce.3.cloned.1.call-start = ((), (), s32[]{:S(2)}) async-start(), calls=%async_computation.3 | async-start | bytes 270336 | tf_op jit(solution)/shard_map/psum | solution.py:11
  7.2 14.2 %copy-start = (f32[16,256,1408]{2,1,0:T(8,128)S(1)}, f32[16,256,1408]{2,1,0:T(8,128)}, u32[]{:S(2)}) copy-start(f32[16,256,1408]{2,1,0:T(8,128)} %param.6) | copy-start | bytes 69206016
  103.5 133.0 %all-to-all-start.1 = ((bf16[16,256,1408]{1,0,2:T(8,128)(2,1)}), bf16[16,256,1408]{1,0,2:T(8,128)(2,1)}, u32[]{:S(2)}, u32[]{:S(2)}) async-start(bf16[16,256,1408]{1,0,2:T(8,128)(2,1)} %divide_convert_fusion), calls=%async_computation.1 | async-start | bytes 23068672 | tf_op jit(solution)/shard_map/all_to_all | solution.py:31
  108.8 23.7 %copy-start.2 = (bf16[16,1408]{1,0:T(8,128)(2,1)S(1)}, bf16[16,1408]{1,0:T(8,128)(2,1)}, u32[]{:S(2)}) copy-start(bf16[16,1408]{1,0:T(8,128)(2,1)} %get-tuple-element.7) | copy-start | bytes 135172
  132.8 109.0 %copy-start.1 = (bf16[16,1408]{1,0:T(8,128)(2,1)S(1)}, bf16[16,1408]{1,0:T(8,128)(2,1)}, u32[]{:S(2)}) copy-start(bf16[16,1408]{1,0:T(8,128)(2,1)} %get-tuple-element.9) | copy-start | bytes 135172
  236.5 133.0 %all-to-all-start = ((bf16[16,256,1408]{1,0,2:T(8,128)(2,1)}), bf16[16,256,1408]{1,0,2:T(8,128)(2,1)}, u32[]{:S(2)}, u32[]{:S(2)}) async-start(bf16[16,256,1408]{1,0,2:T(8,128)(2,1)} %divide_convert_fusion.1), calls=%async_computation | async-start | bytes 23068672 | tf_op jit(solution)/shard_map/all_to_all | solution.py:30
  242.1 132.7 %copy-start.3 = (f32[256,16]{0,1:T(8,128)S(1)}, f32[256,16]{0,1:T(8,128)}, u32[]{:S(2)}) copy-start(f32[256,16]{0,1:T(8,128)} %param.8) | copy-start | bytes 49156
  242.1 132.7 %copy-start.4 = (f32[256]{0:T(256)S(1)}, f32[256]{0:T(256)}, u32[]{:S(2)}) copy-start(f32[256]{0:T(256)} %param.9) | copy-start | bytes 3076
  369.6 211.0 %all-to-all-start.2 = ((bf16[16,1408,256]{2,0,1:T(8,128)(2,1)}), bf16[16,1408,256]{2,0,1:T(8,128)(2,1)}, u32[]{:S(2)}, u32[]{:S(2)}) async-start(bf16[16,1408,256]{2,0,1:T(8,128)(2,1)} %fusion), calls=%async_computation.2 | async-start | bytes 23068672 | tf_op jit(solution)/shard_map/all_to_all | solution.py:33
Sparse Core Ops, SparseCore 0:
  33.2 54.9 all-reduce.2
where the time goes:
time: 620 us; the launch traced here: 617 us
  waiting for transfers between devices  216 us (35%)
  blocking collectives  145 us (23%)
  local copies, waits for them, and re-layouts  144 us (23%)
  other arithmetic  82.7 us (13%)
  starting transfers between devices  15.8 us (3%)
  between operations  14.2 us (2%)
    all_gather x1, blocking collectives, shards(): row_router = lax.all_gather(part_router, 'fsdp', axis=0, tiled=True)  131 us
    all_to_all x1, waiting for transfers between devices, shards(): lax.all_to_all(narrow_gate, 'fsdp', split_axis=2, concat_axis=1, tiled=True)  94.8 us
    all_to_all x1, waiting for transfers between devices, shards(): lax.all_to_all(narrow_up, 'fsdp', split_axis=2, concat_axis=1, tiled=True)  89.5 us
    unnamed x13, local copies, waits for them, and re-layouts  53.1 us
    convert_element_type x1, other arithmetic, shards(): (train_down / jnp.expand_dims(scale_down, 2)).astype(jnp.bfloat16)  32.6 us
    psum x1, waiting for transfers between devices, shards(): lax.psum(jnp.sum(jnp.abs(train_gate), axis=1).astype(jnp.bfloat16), 'fsdp')  31.4 us
    all_to_all x2, local copies, waits for them, and re-layouts, shards(): lax.all_to_all(narrow_gate, 'fsdp', split_axis=2, concat_axis=1, tiled=True)  29.3 us
    all_to_all x2, local copies, waits for them, and re-layouts, shards(): lax.all_to_all(narrow_up, 'fsdp', split_axis=2, concat_axis=1, tiled=True)  29.3 us
  transfers between devices with their start and end apart: 4, of which 3 were waited for; matrix products, arithmetic and copies ran while one was open for 19% of the time, Pallas kernels for 0%

commit v1 on v0

--- a/solution.py
+++ b/solution.py
@@ -30,7 +30,12 @@
         lax.all_to_all(narrow_gate, "fsdp", split_axis=2, concat_axis=1, tiled=True),
         lax.all_to_all(narrow_up, "fsdp", split_axis=2, concat_axis=1, tiled=True),
     )
-    ready_down = lax.all_to_all(narrow_down, "fsdp", split_axis=1, concat_axis=2, tiled=True)
+    ready_down = jnp.concatenate(
+        lax.all_to_all(
+            jnp.stack(jnp.split(narrow_down, lax.axis_size("fsdp"), axis=1)), "fsdp", 0, 0
+        ),
+        axis=2,
+    )
     scale_gate = lax.dynamic_slice_in_dim(
         scale_gate, lax.axis_index("fsdp") * ready_gate.shape[2], ready_gate.shape[2], axis=1
     )

time: 620 us -> 600 us (0.968)
  other arithmetic: 82.7 us -> 59.9 us
  waiting for transfers between devices: 216 us -> 229 us
  local copies, waits for them, and re-layouts: 144 us -> 134 us
    all_to_all x2 -> x0, local copies, waits for them, and re-layouts: 29.3 us -> none  [shards(): lax.all_to_all(narrow_down, 'fsdp', split_axis=1, concat_axis=2, tiled=True)]
    convert_element_type x1, other arithmetic: 32.6 us -> 9.8 us  [shards(): (train_down / jnp.expand_dims(scale_down, 2)).astype(jnp.bfloat16)]
    all_to_all x1, waiting for transfers between devices: 89.5 us -> 108 us  [shards(): lax.all_to_all(narrow_up, 'fsdp', split_axis=2, concat_axis=1, tiled=True)]
    reshape x0 -> x1, local copies, waits for them, and re-layouts: none -> 10 us  [shards(): jnp.concatenate(lax.all_to_all(jnp.stack(jnp.split(narrow_down, lax.axis_...]
    unnamed x13 -> x20, local copies, waits for them, and re-layouts: 53.1 us -> 61.6 us
  transfers between devices with their start and end apart: 4 -> 4, of which waited for: 3 -> 3; matrix products, arithmetic and copies ran while one was open for 19% -> 18% of each run, Pallas kernels for 0% -> 0%
where the time goes in v1:
time: 600 us; the launch traced here: 598 us
  waiting for transfers between devices  229 us (38%)
  blocking collectives  145 us (24%)
  local copies, waits for them, and re-layouts  134 us (22%)
  other arithmetic  59.9 us (10%)
  starting transfers between devices  15.8 us (3%)
  between operations  14.2 us (2%)
    all_gather x1, blocking collectives, shards(): row_router = lax.all_gather(part_router, 'fsdp', axis=0, tiled=True)  131 us
    all_to_all x1, waiting for transfers between devices, shards(): lax.all_to_all(narrow_up, 'fsdp', split_axis=2, concat_axis=1, tiled=True)  108 us
    all_to_all x1, waiting for transfers between devices, shards(): lax.all_to_all(narrow_gate, 'fsdp', split_axis=2, concat_axis=1, tiled=True)  89.6 us
    unnamed x20, local copies, waits for them, and re-layouts  61.6 us
    psum x1, waiting for transfers between devices, shards(): lax.psum(jnp.sum(jnp.abs(train_gate), axis=1).astype(jnp.bfloat16), 'fsdp')  31.4 us
    all_to_all x2, local copies, waits for them, and re-layouts, shards(): lax.all_to_all(narrow_gate, 'fsdp', split_axis=2, concat_axis=1, tiled=True)  29.3 us
    all_to_all x2, local copies, waits for them, and re-layouts, shards(): lax.all_to_all(narrow_up, 'fsdp', split_axis=2, concat_axis=1, tiled=True)  29.3 us
    convert_element_type x1, other arithmetic, shards(): (train_gate / jnp.expand_dims(scale_gate, 1)).astype(jnp.bfloat16)  14.2 us
  transfers between devices with their start and end apart: 4, of which 3 were waited for; matrix products, arithmetic and copies ran while one was open for 18% of the time, Pallas kernels for 0%

profile of v1, /device:TPU:0, one launch (start us, length us, event | category | flops | bytes accessed | tf_op | source)
XLA Modules:
  0.0 598.0 jit_solution(2541055940146341403)
XLA Ops:
  7.2 0.0 all-reduce.3.cloned.1.call-start
  7.2 0.0 copy-start
  7.2 9.2 %abs_reduce_fusion = bf16[16,1408]{1,0:T(8,128)(2,1)} fusion(f32[16,1408,256]{2,1,0:T(8,128)} %param.7), kind=kLoop, calls=%fused_computation.1 | loop fusion | flops 11511808 | bytes 23113728 | tf_op jit(solution)/shard_map/reduce_sum | solution.py:17
  16.4 5.0 copy-done
  21.4 11.7 %abs_reduce_fusion.1 = (bf16[16,1408]{1,0:T(8,128)(2,1)}, bf16[16,1408]{1,0:T(8,128)(2,1)}) fusion(f32[16,256,1408]{2,1,0:T(8,128)} %param.6, f32[16,256,1408]{2,1,0:T(8,128)S(1)} %copy-done), kind=kLoop, calls=%fused_computation.3 | loop fusion | flops 23023616 | bytes 46227456 | tf_op jit(solution)/shard_map/reduce_sum | solution.py:14
  33.1 0.0 all-reduce.3.cloned.1.call-update
  33.1 23.7 %copy.24 = f32[16,256,1408]{1,0,2:T(8,128)} copy(f32[16,256,1408]{2,1,0:T(8,128)} %param.5) | data formatting | bytes 46137344 | tf_op args[0]
  56.8 31.4 %all-reduce.3.cloned.1.call-done = (bf16[16,1408]{1,0:T(8,128)(2,1)}, bf16[16,1408]{1,0:T(8,128)(2,1)}, bf16[16,1408]{1,0:T(8,128)(2,1)}) async-done(((bf16[16,1408]{1,0:T(8,128)(2,1)}, bf16[16,1408]{1,0:T(8,128)(2,1)}, bf16[16,1408]{1,0:T(8,128)(2,1)}), (bf16[16,1408]{1,0:T(8,128)(2,1)}, bf16[16,1408]{1,0:T(8,128)(2,1)}, bf16[16,1408]{1,0:T(8,128)(2,1)})) %all-reduce.3.cloned.1.call-update) | async-done | bytes 135184 | tf_op jit(solution)/shard_map/psum | solution.py:11
  88.3 0.8 convert_multiply_fusion.2
  89.1 0.3 copy.23
  89.3 14.2 %divide_convert_fusion.2 = bf16[16,256,1408]{1,0,2:T(8,128)(2,1)} fusion(f32[16,256,1408]{1,0,2:T(8,128)} %copy.24, f32[16,1408]{0,1:T(8,128)S(1)} %copy.23), kind=kLoop, calls=%fused_computation.4 | loop fusion | flops 11534336 | bytes 34693120 | tf_op jit(solution)/shard_map/convert_element_type | solution.py:25
  103.6 5.2 all-to-all-start
  108.8 0.0 copy-start.2
  108.8 23.7 %copy.28 = f32[16,256,1408]{1,0,2:T(8,128)} copy(f32[16,256,1408]{2,1,0:T(8,128)} %param.6) | data formatting | bytes 46137344 | tf_op args[1]
  132.5 0.0 copy-done.2
  132.5 0.3 copy.27
  132.8 14.2 %divide_convert_fusion.1 = bf16[16,256,1408]{1,0,2:T(8,128)(2,1)} fusion(f32[16,256,1408]{1,0,2:T(8,128)} %copy.28, f32[16,1408]{0,1:T(8,128)S(1)} %copy.27), kind=kLoop, calls=%fused_computation.2 | loop fusion | flops 11534336 | bytes 34693120 | tf_op jit(solution)/shard_map/convert_element_type | solution.py:26
  147.0 0.0 copy-start.1
  147.0 89.6 %all-to-all-done = bf16[16,256,1408]{1,0,2:T(8,128)(2,1)} async-done(((bf16[16,256,1408]{1,0,2:T(8,128)(2,1)}), bf16[16,256,1408]{1,0,2:T(8,128)(2,1)}, u32[]{:S(2)}, u32[]{:S(2)}) %all-to-all-start) | async-done | bytes 11534368 | tf_op jit(solution)/shard_map/all_to_all | solution.py:30
  236.6 5.3 all-to-all-start.1
  241.8 0.0 copy-done.1
  241.9 9.8 %divide_convert_fusion = bf16[16,1408,256]{2,1,0:T(8,128)(2,1)S(1)} fusion(f32[16,1408,256]{2,1,0:T(8,128)} %param.7, f32[16,1408]{1,0:T(8,128)S(1)} %convert_multiply_fusion), kind=kLoop, calls=%fused_computation | loop fusion | flops 11534336 | bytes 34693120 | tf_op jit(solution)/shard_map/convert_element_type | solution.py:27
  251.7 1.2 fusion.7
  252.8 1.2 fusion.6
  254.1 1.2 fusion.5
  255.3 1.2 fusion.4
  256.5 1.2 fusion.3
  257.6 1.2 fusion.2
  258.9 1.2 fusion.1
  260.1 1.2 fusion
  261.3 0.0 copy-start.3
  261.3 0.0 copy-start.4
  261.3 108.3 %all-to-all-done.1 = bf16[16,256,1408]{1,0,2:T(8,128)(2,1)} async-done(((bf16[16,256,1408]{1,0,2:T(8,128)(2,1)}), bf16[16,256,1408]{1,0,2:T(8,128)(2,1)}, u32[]{:S(2)}, u32[]{:S(2)}) %all-to-all-start.1) | async-done | bytes 11534368 | tf_op jit(solution)/shard_map/all_to_all | solution.py:31
  369.6 5.3 all-to-all-start.2
  374.9 0.0 copy-done.3
  374.9 0.0 copy-done.4
  374.9 130.9 %all_gather.6 = bf16[2048,16]{0,1:T(8,128)(2,1)S(1)} all-gather(bf16[256,16]{0,1:T(8,128)(2,1)S(1)} %multiply_convert_fusion), channel_id=1, replica_groups=mesh['ep'=4,'fsdp'=8] {'fsdp'}, dimensions={0}, use_global_device_ids=true | all-gather | bytes 73728 | tf_op jit(solution)/shard_map/all_gather | solution.py:49
  505.8 14.0 %all_gather.7 = bf16[2048,64]{0,1:T(8,128)(2,1)S(1)} all-gather(bf16[2048,16]{0,1:T(8,128)(2,1)S(1)} %all_gather.6), channel_id=1, replica_groups=mesh['ep'=4,'fsdp'=8] {'ep'}, dimensions={1}, use_global_device_ids=true | all-gather | bytes 327680 | tf_op jit(solution)/shard_map/all_gather | solution.py:50
  519.8 0.7 constant_dynamic-slice_fusion.2
  520.5 0.7 constant_dynamic-slice_fusion.1
  521.1 0.7 constant_dynamic-slice_fusion
  521.8 11.3 %copy.26 = bf16[16,8,256,176]{2,1,3,0:T(8,128)(2,1)} copy(bf16[16,8,256,176]{2,0,3,1:T(8,128)(2,1)} %bitcast.2) | data formatting | bytes 23068672 | tf_op jit(solution)/shard_map/all_to_all | solution.py:30
  533.1 18.0 %all_to_all.32 = bf16[16,2048,176]{1,2,0:T(8,128)(2,1)} reshape(bf16[16,8,256,176]{2,1,3,0:T(8,128)(2,1)} %copy.26) | data formatting | bytes 23068672 | tf_op jit(solution)/shard_map/all_to_all | solution.py:30
  551.1 11.3 %copy.30 = bf16[16,8,256,176]{2,1,3,0:T(8,128)(2,1)} copy(bf16[16,8,256,176]{2,0,3,1:T(8,128)(2,1)} %bitcast.5) | data formatting | bytes 23068672 | tf_op jit(solution)/shard_map/all_to_all | solution.py:31
  562.4 18.0 %all_to_all.36 = bf16[16,2048,176]{1,2,0:T(8,128)(2,1)} reshape(bf16[16,8,256,176]{2,1,3,0:T(8,128)(2,1)} %copy.30) | data formatting | bytes 23068672 | tf_op jit(solution)/shard_map/all_to_all | solution.py:31
  580.4 0.0 all-to-all-done.2
  580.4 10.0 %copy.34 = bf16[8,16,22,8,256]{4,3,0,2,1:T(8,128)(2,1)} copy(bf16[8,16,22,8,256]{4,3,2,1,0:T(8,128)(2,1)} %bitcast.15) | data formatting | bytes 23068672 | tf_op jit(solution)/shard_map/reshape | solution.py:33
  590.4 0.7 copy.46
  (3 shorter events, 0.0 us)
Async XLA Ops:
  7.2 81.1 %all-reduce.3.cloned.1.call-start = ((), (), s32[]{:S(2)}) async-start(), calls=%async_computation.3 | async-start | bytes 270336 | tf_op jit(solution)/shard_map/psum | solution.py:11
  7.2 14.2 %copy-start = (f32[16,256,1408]{2,1,0:T(8,128)S(1)}, f32[16,256,1408]{2,1,0:T(8,128)}, u32[]{:S(2)}) copy-start(f32[16,256,1408]{2,1,0:T(8,128)} %param.5) | copy-start | bytes 69206016
  103.6 133.0 %all-to-all-start = ((bf16[16,256,1408]{1,0,2:T(8,128)(2,1)}), bf16[16,256,1408]{1,0,2:T(8,128)(2,1)}, u32[]{:S(2)}, u32[]{:S(2)}) async-start(bf16[16,256,1408]{1,0,2:T(8,128)(2,1)} %divide_convert_fusion.2), calls=%async_computation | async-start | bytes 23068672 | tf_op jit(solution)/shard_map/all_to_all | solution.py:30
  108.8 23.7 %copy-start.2 = (bf16[16,1408]{1,0:T(8,128)(2,1)S(1)}, bf16[16,1408]{1,0:T(8,128)(2,1)}, u32[]{:S(2)}) copy-start(bf16[16,1408]{1,0:T(8,128)(2,1)} %get-tuple-element.8) | copy-start | bytes 135172
  147.0 94.8 %copy-start.1 = (bf16[16,1408]{1,0:T(8,128)(2,1)S(1)}, bf16[16,1408]{1,0:T(8,128)(2,1)}, u32[]{:S(2)}) copy-start(bf16[16,1408]{1,0:T(8,128)(2,1)} %get-tuple-element.9) | copy-start | bytes 135172
  236.6 133.0 %all-to-all-start.1 = ((bf16[16,256,1408]{1,0,2:T(8,128)(2,1)}), bf16[16,256,1408]{1,0,2:T(8,128)(2,1)}, u32[]{:S(2)}, u32[]{:S(2)}) async-start(bf16[16,256,1408]{1,0,2:T(8,128)(2,1)} %divide_convert_fusion.1), calls=%async_computation.1 | async-start | bytes 23068672 | tf_op jit(solution)/shard_map/all_to_all | solution.py:31
  261.3 113.6 %copy-start.3 = (f32[256,16]{0,1:T(8,128)S(1)}, f32[256,16]{0,1:T(8,128)}, u32[]{:S(2)}) copy-start(f32[256,16]{0,1:T(8,128)} %param.8) | copy-start | bytes 49156
  261.3 113.6 %copy-start.4 = (f32[256]{0:T(256)S(1)}, f32[256]{0:T(256)}, u32[]{:S(2)}) copy-start(f32[256]{0:T(256)} %param.9) | copy-start | bytes 3076
  369.6 210.8 %all-to-all-start.2 = ((bf16[8,16,176,256]{3,2,1,0:T(8,128)(2,1)}), bf16[8,16,176,256]{3,2,1,0:T(8,128)(2,1)}, u32[]{:S(2)}, u32[]{:S(2)}) async-start(bf16[8,16,176,256]{3,2,1,0:T(8,128)(2,1)} %fusion), calls=%async_computation.2 | async-start | bytes 23068672 | tf_op jit(solution)/shard_map/all_to_all | solution.py:34
Sparse Core Ops, SparseCore 0:
  33.3 54.9 all-reduce.2
